TPU v7x, 32 devices: a whole 2x2x4 slice. The times are simulated.
32 devices in a mesh: rows: 2 (over core), cols: 2 (over y), slabs: 2 (over x), site: 4 (over z).
Axes of the slice: x: 2, y: 2, z: 4, core: 2. Of those that a mesh axis runs over, the one named last changes fastest.
Arguments:
- field_values: float32 [768, 16, 16, 128], P(('site', 'rows'), 'cols', 'slabs'), parts along dimension 0, may hold values from 0.5 to 2
- crowding: float32 [768, 16, 16, 128], P(('site', 'rows'), 'cols', 'slabs'), parts along dimension 0, may hold values from 0.5 to 2
Outputs:
- standardized: float32 [768, 16, 16, 128], P(('site', 'rows'), 'cols', 'slabs'), parts along dimension 0
- field_values_end: float32 [768, 16, 16, 128], P(('site', 'rows'), 'cols', 'slabs'), parts along dimension 0
There are 4 independent parts, one for each index of `site`. A program takes and returns all parts, laid end to end along the dimension named above; each array names one. Nothing has to cross between parts.
All inputs are finite; a program needn't handle non-finite values.
Results may differ from a plain program's by a relative error of at most 0.000036.
Values sent between devices are 32-bit elements; how exact they have to be, the bound alone decides.
A program may use at most 64 MiB of HBM per device.

v0:
```python
import functools

import jax
import jax.numpy as jnp
from jax import lax
from jax.experimental import pallas as pl
from jax.experimental.pallas import tpu as pltpu
from jax.sharding import PartitionSpec as P

MESH = pl.DeviceIdType.MESH
STEPS = 6


def ring(axis, devices):
    me = lax.axis_index(axis)
    return lax.rem(me + 1, devices), lax.rem(me + devices - 1, devices)


def kernel(dims, f_hbm, c_hbm, end, mean_out, scale_out, fbuf, cbuf, xsend, xrecv, zsend, zrecv, moments,
           load_sem, crowd_sem, face_send, face_recv, row_send, row_recv, mom_send, mom_recv):
    rows, cols, slabs, size_y, size_x, size_z, chunks = dims
    ny = size_y // chunks
    levels = f_hbm.shape[-1]
    x_next = ring("cols", cols)
    z_next = ring("slabs", slabs)
    x_copies = 1 if cols == 2 else 2
    y_next = ring("rows", rows)
    tile = [pl.ds(x * size_z, size_z) for x in range(size_x)]

    def inner(j):
        return pl.ds(j * ny + 1, ny)

    def outer(j):
        return pl.ds(j * ny, ny)

    def faces(k, j):
        copies = []
        for at, (axis, devices, source, target, peers) in enumerate((
                ("cols", cols, xsend, xrecv, x_next), ("slabs", slabs, zsend, zrecv, z_next))):
            for side in range(1 if devices == 2 else 2):
                sides = pl.ds(side, 2 if devices == 2 else 1)
                copies.append(pltpu.make_async_remote_copy(
                    src_ref=source.at[k, sides, outer(j)], dst_ref=target.at[k, sides, outer(j)],
                    send_sem=face_send.at[k, j, 2 * at + side], recv_sem=face_recv.at[k, j, 2 * at + side],
                    device_id={axis: peers[side]}, device_id_type=MESH))
        return copies

    def y_copy(k, side):
        return pltpu.make_async_remote_copy(
            src_ref=fbuf.at[k, size_y if side == 0 else 1],
            dst_ref=fbuf.at[k, 0 if side == 0 else size_y + 1],
            send_sem=row_send.at[k, side], recv_sem=row_recv.at[k, side],
            device_id={"rows": y_next[side]}, device_id_type=MESH)

    def load(j):
        return pltpu.make_async_copy(f_hbm.at[outer(j)], fbuf.at[0, inner(j)], load_sem.at[j])

    def load_face(side):
        return pltpu.make_async_copy(
            f_hbm.at[:, tile[size_x - 1 if side == 0 else 0]], xsend.at[0, side], load_sem.at[chunks + side])

    crowd = pltpu.make_async_copy(c_hbm, cbuf, crowd_sem)

    def moment_copy(r):
        return pltpu.make_async_remote_copy(
            src_ref=moments.at[0], dst_ref=moments.at[r],
            send_sem=mom_send.at[r], recv_sem=mom_recv.at[r],
            device_id={"rows": lax.rem(lax.axis_index("rows") + r, rows)}, device_id_type=MESH)

    def start_faces(k, j):
        copies = faces(k, j)
        for copy in copies[:x_copies]:
            copy.start()

        @pl.when(j == 0)
        def _():
            y_copy(k, 1).start()

        @pl.when(j == chunks - 1)
        def _():
            y_copy(k, 0).start()

        @pl.loop(0, ny)
        def _(r):
            y = j * ny + r
            for side in (0, 1):
                first = size_z - 1 if side == 0 else 0
                zsend[k, side, y] = fbuf[k, y + 1, pl.ds(first, size_x, stride=size_z), :]

        for copy in copies[x_copies:]:
            copy.start()

    def wait_faces(k, j, recv):
        for copy in faces(k, j):
            if recv:
                copy.wait_recv()
            else:
                copy.wait_send()

        for side, at in ((0, 0 if recv else chunks - 1), (1, chunks - 1 if recv else 0)):
            @pl.when(j == at)
            def _():
                if recv:
                    y_copy(k, side).wait_recv()
                else:
                    y_copy(k, side).wait_send()

    at_z = lax.broadcasted_iota(jnp.int32, (size_z, levels), 0)

    def advance(k, j, sums):
        def row(r, sums):
            y = j * ny + r
            mid = [fbuf[k, y + 1, tile[x], :] for x in range(size_x)]
            out = []
            for x in range(size_x):
                m = mid[x]
                below = mid[x - 1] if x > 0 else xrecv[k, 0, y]
                above = mid[x + 1] if x < size_x - 1 else xrecv[k, 1, y]
                z_lo = jnp.broadcast_to(zrecv[k, 0, y, pl.ds(x, 1), :], m.shape)
                z_hi = jnp.broadcast_to(zrecv[k, 1, y, pl.ds(x, 1), :], m.shape)
                left = jnp.where(at_z == 0, z_lo, pltpu.roll(m, 1, 0))
                right = jnp.where(at_z == size_z - 1, z_hi, pltpu.roll(m, size_z - 1, 0))
                near = (fbuf[k, y, tile[x], :] + fbuf[k, y + 2, tile[x], :]) + (below + above) + (left + right)
                new = 0.1 * near + m * (0.6 - 0.2 * (m * cbuf[y, tile[x], :]))
                if sums:
                    end[y, tile[x], :] = new
                else:
                    fbuf[k + 1, y + 1, tile[x], :] = new
                    if x == size_x - 1:
                        xsend[k + 1, 0, y] = new
                    if x == 0:
                        xsend[k + 1, 1, y] = new
                out.append(new)
            return tuple(s + o for s, o in zip(sums, out)) if sums else ()

        return lax.fori_loop(0, ny, row, sums)

    load(0).start()
    for side in (0, 1):
        load_face(side).start()

    barrier = pltpu.get_barrier_semaphore()
    count = 0
    for axis, devices, peers in (("cols", cols, x_next), ("slabs", slabs, z_next)):
        for peer in peers[:1 if devices == 2 else 2]:
            pl.semaphore_signal(barrier, inc=1, device_id={axis: peer}, device_id_type=MESH)
            count += 1
    for r in range(1, rows):
        pl.semaphore_signal(barrier, inc=1, device_id={"rows": lax.rem(lax.axis_index("rows") + r, rows)}, device_id_type=MESH)
        count += 1
    pl.semaphore_wait(barrier, count)

    for j in range(1, chunks):
        load(j).start()
    for side in (0, 1):
        load_face(side).wait()

    @pl.loop(0, chunks)
    def _(j):
        load(j).wait()
        start_faces(0, j)

    crowd.start()
    crowd.wait()
    moments[0] = jnp.zeros(moments.shape[1:], jnp.float32)

    @pl.loop(0, STEPS - 1)
    def _(k):
        @pl.loop(0, chunks)
        def _(i):
            j = lax.rem(k + i, chunks)
            wait_faces(k, j, True)
            advance(k, j, ())
            start_faces(k + 1, j)
            wait_faces(k, j, False)

    last = STEPS - 1
    zero = jnp.zeros((size_z, levels), jnp.float32)

    @pl.loop(0, chunks)
    def _(i):
        j = lax.rem(last - 1 + i, chunks)
        wait_faces(last, j, True)
        sums = advance(last, j, (zero,) * size_x)
        means = tuple(s * (1.0 / ny) for s in sums)

        def spread(r, squares):
            deltas = [end[j * ny + r, tile[x], :] - means[x] for x in range(size_x)]
            return tuple(s + d * d for s, d in zip(squares, deltas))

        squares = lax.fori_loop(0, ny, spread, (zero,) * size_x)
        share = 1.0 / (i + 1).astype(jnp.float32)
        weight = i.astype(jnp.float32) * share * ny
        for x in range(size_x):
            delta = means[x] - moments[0, 0, tile[x], :]
            moments[0, 0, tile[x], :] += delta * share
            moments[0, 1, tile[x], :] += squares[x] + delta * delta * weight

    for r in range(1, rows):
        moment_copy(r).start()
    for r in range(1, rows):
        moment_copy(r).wait_recv()
    for x in range(size_x):
        parts = [moments[r, 0, tile[x], :] for r in range(rows)]
        mean = sum(parts[1:], parts[0]) * (1.0 / rows)
        square = sum([moments[r, 1, tile[x], :] for r in range(1, rows)], moments[0, 1, tile[x], :])
        for p in parts:
            square = square + size_y * ((p - mean) * (p - mean))
        mean_out[tile[x], :] = mean
        scale_out[tile[x], :] = lax.rsqrt(square * (1.0 / (rows * size_y)) + 0.0001)

    for r in range(1, rows):
        moment_copy(r).wait_send()

    @pl.loop(0, chunks)
    def _(j):
        wait_faces(last, j, False)


def local(dims, field_values, crowding):
    shape = field_values.shape
    size_y, size_x, size_z, levels = shape
    rows, cols, slabs = dims
    chunks = next(n for n in (4, 3, 6, 2, 1) if size_y % n == 0)
    flat = (size_y, size_x * size_z, levels)
    dma = pltpu.SemaphoreType.DMA
    out = tuple(pltpu.VMEM(each, jnp.float32) for each in (flat, flat[1:], flat[1:]))
    vmem_spec = pl.BlockSpec(memory_space=pltpu.VMEM)
    any_spec = pl.BlockSpec(memory_space=pl.ANY)
    field_end, mean, scale = pl.pallas_call(
        functools.partial(kernel, (rows, cols, slabs, size_y, size_x, size_z, chunks)),
        out_shape=out,
        in_specs=[any_spec] * 2,
        out_specs=(vmem_spec,) * 3,
        scratch_shapes=[
            pltpu.VMEM((STEPS, size_y + 2, size_x * size_z, levels), jnp.float32),
            pltpu.VMEM(flat, jnp.float32),
            pltpu.VMEM((STEPS, 2, size_y, size_z, levels), jnp.float32),
            pltpu.VMEM((STEPS, 2, size_y, size_z, levels), jnp.float32),
            pltpu.VMEM((STEPS, 2, size_y, size_x, levels), jnp.float32),
            pltpu.VMEM((STEPS, 2, size_y, size_x, levels), jnp.float32),
            pltpu.VMEM((rows, 2, size_x * size_z, levels), jnp.float32),
            dma((chunks + 2,)),
            dma,
            dma((STEPS, chunks, 4)),
            dma((STEPS, chunks, 4)),
            dma((STEPS, 2)),
            dma((STEPS, 2)),
            dma((rows,)),
            dma((rows,)),
        ],
        compiler_params=pltpu.CompilerParams(
            collective_id=0, has_side_effects=True, vmem_limit_bytes=58 * 1024 * 1024),
    )(field_values.reshape(flat), crowding.reshape(flat))
    field_end = field_end.reshape(shape)
    return (field_end - mean.reshape(shape[1:])) * scale.reshape(shape[1:]), field_end


def solution(mesh):
    spec = P(("site", "rows"), "cols", "slabs", None)
    dims = tuple(mesh.shape[axis] for axis in ("rows", "cols", "slabs"))
    return jax.shard_map(
        functools.partial(local, dims), mesh=mesh,
        in_specs=(spec, spec), out_specs=(spec, spec), check_vma=False)
```

profile of v0, /device:TPU:0, one launch (start us, length us, event | category | flops | bytes accessed | tf_op | source)
XLA Modules:
  0.0 114.8 jit_solution(12133806685419371675)
XLA Ops:
  0.6 110.2 %shard_map.41 = (f32[96,64,128]{2,1,0:T(8,128)S(1)}, f32[64,128]{1,0:T(8,128)S(1)}, f32[64,128]{1,0:T(8,128)S(1)}) custom-call(f32[96,64,128]{2,1,0:T(8,128)} %bitcast.9, f32[96,64,128]{2,1,0:T(8,128)} %bitcast.10), custom_call_target="tpu_custom_call" | custom-call | tf_op jit(solution)/shard_map/pallas_call | solution.py:230
  110.8 2.3 %subtract_multiply_fusion = f32[96,8,8,128]{3,2,1,0:T(8,128)} fusion(f32[8,8,128]{2,1,0:T(8,128)S(1)} %bitcast.8, f32[8,8,128]{2,1,0:T(8,128)S(1)} %bitcast.7, f32[96,64,128]{2,1,0:T(8,128)S(1)} %get-tuple-element.5), kind=kLoop, calls=%fused_computation | loop fusion | flops 1572864 | bytes 6356992 | tf_op jit(solution)/shard_map/mul | solution.py:256
  113.1 1.7 %copy.5 = f32[96,8,8,128]{3,2,1,0:T(8,128)} copy(f32[96,8,8,128]{3,2,1,0:T(8,128)S(1)} %bitcast.6) | data formatting | bytes 6291456
where the time goes:
time: 115 us
  Pallas kernels  110 us (96%)
  other arithmetic  2.33 us (2%)
  local copies, waits for them, and re-layouts  1.66 us (1%)
    pallas_call x1, Pallas kernels, local(): pl.pallas_call(functools.partial(kernel, (rows, cols, slabs, size_y, size...  110 us
    mul x1, other arithmetic, local(): (field_end - mean.reshape(shape[1:])) * scale.reshape(shape[1:])  2.33 us

commit v1 on v0

--- a/solution.py
+++ b/solution.py
@@ -16,7 +16,7 @@
     return lax.rem(me + 1, devices), lax.rem(me + devices - 1, devices)
 
 
-def kernel(dims, f_hbm, c_hbm, end, mean_out, scale_out, fbuf, cbuf, xsend, xrecv, zsend, zrecv, moments,
+def kernel(dims, f_hbm, c_hbm, end, moments, fbuf, cbuf, xsend, xrecv, zsend, zrecv,
            load_sem, crowd_sem, face_send, face_recv, row_send, row_recv, mom_send, mom_recv):
     rows, cols, slabs, size_y, size_x, size_z, chunks = dims
     ny = size_y // chunks
@@ -200,21 +200,42 @@
         moment_copy(r).start()
     for r in range(1, rows):
         moment_copy(r).wait_recv()
-    for x in range(size_x):
-        parts = [moments[r, 0, tile[x], :] for r in range(rows)]
-        mean = sum(parts[1:], parts[0]) * (1.0 / rows)
-        square = sum([moments[r, 1, tile[x], :] for r in range(1, rows)], moments[0, 1, tile[x], :])
-        for p in parts:
-            square = square + size_y * ((p - mean) * (p - mean))
-        mean_out[tile[x], :] = mean
-        scale_out[tile[x], :] = lax.rsqrt(square * (1.0 / (rows * size_y)) + 0.0001)
-
     for r in range(1, rows):
         moment_copy(r).wait_send()
 
     @pl.loop(0, chunks)
     def _(j):
         wait_faces(last, j, False)
+
+
+def finish(size_y, end, moments, standardized_hbm, end_hbm, out, end_sem, out_sem):
+    rows = moments.shape[0]
+    pieces = out_sem.shape[0]
+    ny = size_y // pieces
+    copy_end = pltpu.make_async_copy(end, end_hbm, end_sem)
+    copy_end.start()
+
+    parts = [moments[r, 0] for r in range(rows)]
+    mean = sum(parts[1:], parts[0]) * (1.0 / rows)
+    square = sum([moments[r, 1] for r in range(1, rows)], moments[0, 1])
+    for p in parts:
+        square = square + size_y * ((p - mean) * (p - mean))
+    scale = lax.rsqrt(square * (1.0 / (rows * size_y)) + 0.0001)
+
+    def store(j):
+        return pltpu.make_async_copy(out.at[pl.ds(j * ny, ny)], standardized_hbm.at[pl.ds(j * ny, ny)], out_sem.at[j])
+
+    for j in range(pieces):
+        @pl.loop(0, ny)
+        def _(r):
+            y = j * ny + r
+            out[y] = (end[y] - mean) * scale
+
+        store(j).start()
+
+    for j in range(pieces):
+        store(j).wait()
+    copy_end.wait()
 
 
 def local(dims, field_values, crowding):
@@ -224,14 +245,15 @@
     chunks = next(n for n in (4, 3, 6, 2, 1) if size_y % n == 0)
     flat = (size_y, size_x * size_z, levels)
     dma = pltpu.SemaphoreType.DMA
-    out = tuple(pltpu.VMEM(each, jnp.float32) for each in (flat, flat[1:], flat[1:]))
+    held = (flat, (rows, 2) + flat[1:])
+    out = tuple(pltpu.VMEM(each, jnp.float32) for each in held)
     vmem_spec = pl.BlockSpec(memory_space=pltpu.VMEM)
     any_spec = pl.BlockSpec(memory_space=pl.ANY)
-    field_end, mean, scale = pl.pallas_call(
+    field_end, moments = pl.pallas_call(
         functools.partial(kernel, (rows, cols, slabs, size_y, size_x, size_z, chunks)),
         out_shape=out,
         in_specs=[any_spec] * 2,
-        out_specs=(vmem_spec,) * 3,
+        out_specs=(vmem_spec,) * 2,
         scratch_shapes=[
             pltpu.VMEM((STEPS, size_y + 2, size_x * size_z, levels), jnp.float32),
             pltpu.VMEM(flat, jnp.float32),
@@ -239,7 +261,6 @@
             pltpu.VMEM((STEPS, 2, size_y, size_z, levels), jnp.float32),
             pltpu.VMEM((STEPS, 2, size_y, size_x, levels), jnp.float32),
             pltpu.VMEM((STEPS, 2, size_y, size_x, levels), jnp.float32),
-            pltpu.VMEM((rows, 2, size_x * size_z, levels), jnp.float32),
             dma((chunks + 2,)),
             dma,
             dma((STEPS, chunks, 4)),
@@ -252,8 +273,16 @@
         compiler_params=pltpu.CompilerParams(
             collective_id=0, has_side_effects=True, vmem_limit_bytes=58 * 1024 * 1024),
     )(field_values.reshape(flat), crowding.reshape(flat))
-    field_end = field_end.reshape(shape)
-    return (field_end - mean.reshape(shape[1:])) * scale.reshape(shape[1:]), field_end
+    whole = jax.ShapeDtypeStruct(flat, jnp.float32)
+    standardized, field_end = pl.pallas_call(
+        functools.partial(finish, size_y),
+        out_shape=(whole, whole),
+        in_specs=[vmem_spec] * 2,
+        out_specs=(any_spec,) * 2,
+        scratch_shapes=[pltpu.VMEM(flat, jnp.float32), dma, dma((chunks,))],
+        compiler_params=pltpu.CompilerParams(vmem_limit_bytes=16 * 1024 * 1024),
+    )(*(pltpu.with_memory_space_constraint(each, pltpu.VMEM) for each in (field_end, moments)))
+    return standardized.reshape(shape), field_end.reshape(shape)
 
 
 def solution(mesh):

time: 115 us -> 114 us (level)
  Pallas kernels: 110 us -> 113 us
  other arithmetic: 2.33 us -> 0 us
  local copies, waits for them, and re-layouts: 1.66 us -> 0 us
    pallas_call x0 -> x1, Pallas kernels: none -> 2.72 us  [local(): pl.pallas_call(functools.partial(finish, size_y), out_shape=(whole, whole...]
    mul x1 -> x0, other arithmetic: 2.33 us -> none  [local(): (field_end - mean.reshape(shape[1:])) * scale.reshape(shape[1:])]
    unnamed x1 -> x0, local copies, waits for them, and re-layouts: 1.66 us -> none
where the time goes in v1:
time: 114 us
  Pallas kernels  113 us (99%)
    pallas_call x1, Pallas kernels, local(): pl.pallas_call(functools.partial(kernel, (rows, cols, slabs, size_y, size...  110 us
    pallas_call x1, Pallas kernels, local(): pl.pallas_call(functools.partial(finish, size_y), out_shape=(whole, whole...  2.72 us

profile of v1, /device:TPU:0, one launch (start us, length us, event | category | flops | bytes accessed | tf_op | source)
XLA Modules:
  0.0 113.5 jit_solution(4589849436707307826)
XLA Ops:
  0.6 110.2 %shard_map.41 = (f32[96,64,128]{2,1,0:T(8,128)S(1)}, f32[2,2,64,128]{3,2,1,0:T(8,128)S(1)}) custom-call(f32[96,64,128]{2,1,0:T(8,128)} %bitcast.4, f32[96,64,128]{2,1,0:T(8,128)} %bitcast.5), custom_call_target="tpu_custom_call" | custom-call | tf_op jit(solution)/shard_map/pallas_call | solution.py:252
  110.8 2.7 %shard_map.42 = (f32[96,64,128]{2,1,0:T(8,128)}, f32[96,64,128]{2,1,0:T(8,128)}) custom-call(f32[96,64,128]{2,1,0:T(8,128)S(1)} %get-tuple-element.6.end, f32[2,2,64,128]{3,2,1,0:T(8,128)S(1)} %get-tuple-element.7.moments), custom_call_target="tpu_custom_call" | custom-call | tf_op jit(solution)/shard_map/pallas_call | solution.py:277

commit v2 on v1

v2 whole, which is shorter than its diff:
```python
import functools

import jax
import jax.numpy as jnp
from jax import lax
from jax.experimental import pallas as pl
from jax.experimental.pallas import tpu as pltpu
from jax.sharding import PartitionSpec as P

MESH = pl.DeviceIdType.MESH
STEPS = 6


def ring(axis, devices):
    me = lax.axis_index(axis)
    return lax.rem(me + 1, devices), lax.rem(me + devices - 1, devices)


def pieces_of(size_y):
    small = max(1, size_y // 12)

    def cut(*ends):
        ends = sorted({e for e in ends if 0 < e < size_y} | {0, size_y})
        return tuple((lo, hi - lo) for lo, hi in zip(ends, ends[1:]))

    middle = tuple(size_y * i // 2 for i in range(1, 2))
    first = cut(small, *middle)
    last = cut(size_y - small, *middle)
    return (first,) + (cut(*middle),) * (STEPS - 2) + (last,)


def kernel(dims, f_hbm, c_hbm, end, moments, fbuf, cbuf, xsend, xrecv, zsend, zrecv,
           load_sem, crowd_sem, face_send, face_recv, row_send, row_recv, mom_send, mom_recv):
    rows, cols, slabs, size_y, size_x, size_z = dims
    pieces = pieces_of(size_y)
    levels = f_hbm.shape[-1]
    x_next = ring("cols", cols)
    z_next = ring("slabs", slabs)
    x_copies = 1 if cols == 2 else 2
    y_next = ring("rows", rows)
    tile = [pl.ds(x * size_z, size_z) for x in range(size_x)]

    def faces(k, p):
        copies = []
        at_rows = pl.ds(*pieces[k][p])
        for axis, devices, source, target, peers in (
                ("cols", cols, xsend, xrecv, x_next), ("slabs", slabs, zsend, zrecv, z_next)):
            for side in range(1 if devices == 2 else 2):
                sides = pl.ds(side, 2 if devices == 2 else 1)
                copies.append(pltpu.make_async_remote_copy(
                    src_ref=source.at[k, sides, at_rows], dst_ref=target.at[k, sides, at_rows],
                    send_sem=face_send.at[len(copies)], recv_sem=face_recv.at[k % 2, p, len(copies)],
                    device_id={axis: peers[side]}, device_id_type=MESH))
        return copies

    def y_copy(k, side):
        return pltpu.make_async_remote_copy(
            src_ref=fbuf.at[k, size_y if side == 0 else 1],
            dst_ref=fbuf.at[k, 0 if side == 0 else size_y + 1],
            send_sem=row_send, recv_sem=row_recv.at[k % 2, side],
            device_id={"rows": y_next[side]}, device_id_type=MESH)

    def load(p):
        lo, ny = pieces[0][p]
        return pltpu.make_async_copy(f_hbm.at[pl.ds(lo, ny)], fbuf.at[0, pl.ds(lo + 1, ny)], load_sem.at[p])

    crowd = pltpu.make_async_copy(c_hbm, cbuf, crowd_sem)

    def moment_copy(r):
        return pltpu.make_async_remote_copy(
            src_ref=moments.at[0], dst_ref=moments.at[r],
            send_sem=mom_send.at[r - 1], recv_sem=mom_recv.at[r - 1],
            device_id={"rows": lax.rem(lax.axis_index("rows") + r, rows)}, device_id_type=MESH)

    def start_faces(k, p):
        lo, ny = pieces[k][p]
        copies = faces(k, p)
        if k:
            for copy in copies[:x_copies]:
                copy.start()

        @pl.loop(0, ny)
        def _(r):
            y = lo + r
            for side in (0, 1):
                first = size_z - 1 if side == 0 else 0
                zsend[k, side, y] = fbuf[k, y + 1, pl.ds(first, size_x, stride=size_z), :]
                if not k:
                    xsend[k, side, y] = fbuf[k, y + 1, tile[size_x - 1 if side == 0 else 0], :]

        for copy in copies[x_copies if k else 0:]:
            copy.start()

    def start_y(k, p):
        lo, ny = pieces[k][p]
        if lo == 0:
            y_copy(k, 1).start()
        if lo + ny == size_y:
            y_copy(k, 0).start()

    def wait_recv(k, p):
        lo, ny = pieces[k][p]
        for copy in faces(k, p):
            copy.wait_recv()
        if lo == 0:
            y_copy(k, 0).wait_recv()
        if lo + ny == size_y:
            y_copy(k, 1).wait_recv()

    at_z = lax.broadcasted_iota(jnp.int32, (size_z, levels), 0)

    def advance(k, p, sums):
        lo, ny = pieces[k][p]

        def row(r, sums):
            y = lo + r
            mid = [fbuf[k, y + 1, tile[x], :] for x in range(size_x)]
            out = []
            for x in range(size_x):
                m = mid[x]
                below = mid[x - 1] if x > 0 else xrecv[k, 0, y]
                above = mid[x + 1] if x < size_x - 1 else xrecv[k, 1, y]
                z_lo = jnp.broadcast_to(zrecv[k, 0, y, pl.ds(x, 1), :], m.shape)
                z_hi = jnp.broadcast_to(zrecv[k, 1, y, pl.ds(x, 1), :], m.shape)
                left = jnp.where(at_z == 0, z_lo, pltpu.roll(m, 1, 0))
                right = jnp.where(at_z == size_z - 1, z_hi, pltpu.roll(m, size_z - 1, 0))
                near = (fbuf[k, y, tile[x], :] + fbuf[k, y + 2, tile[x], :]) + (below + above) + (left + right)
                new = 0.1 * near + m * (0.6 - 0.2 * (m * cbuf[y, tile[x], :]))
                if sums:
                    end[y, tile[x], :] = new
                else:
                    fbuf[k + 1, y + 1, tile[x], :] = new
                    if x == size_x - 1:
                        xsend[k + 1, 0, y] = new
                    if x == 0:
                        xsend[k + 1, 1, y] = new
                out.append(new)
            return tuple(s + o for s, o in zip(sums, out)) if sums else ()

        return lax.fori_loop(0, ny, row, sums)

    load(0).start()

    barrier = pltpu.get_barrier_semaphore()
    count = 0
    for axis, devices, peers in (("cols", cols, x_next), ("slabs", slabs, z_next)):
        for peer in peers[:1 if devices == 2 else 2]:
            pl.semaphore_signal(barrier, inc=1, device_id={axis: peer}, device_id_type=MESH)
            count += 1
    for r in range(1, rows):
        pl.semaphore_signal(barrier, inc=1, device_id={"rows": lax.rem(lax.axis_index("rows") + r, rows)}, device_id_type=MESH)
        count += 1

    load(1).start()
    pl.semaphore_wait(barrier, count)

    for p in range(len(pieces[0])):
        if p + 2 < len(pieces[0]):
            load(p + 2).start()
        load(p).wait()
        start_faces(0, p)
        start_y(0, p)
    crowd.start()
    crowd.wait()

    last = STEPS - 1
    for k in range(last):
        sent, ready = set(), 0
        for p, (lo, ny) in enumerate(pieces[k]):
            wait_recv(k, p)
            advance(k, p, ())
            ready = lo + ny
            for q, (q_lo, q_ny) in enumerate(pieces[k + 1]):
                if q not in sent and q_lo + q_ny <= ready:
                    sent.add(q)
                    start_faces(k + 1, q)
                    start_y(k + 1, q)

    zero = jnp.zeros((size_z, levels), jnp.float32)
    done = 0
    for p, (lo, ny) in enumerate(pieces[last]):
        wait_recv(last, p)
        sums = advance(last, p, (zero,) * size_x)
        means = tuple(s * (1.0 / ny) for s in sums)

        def spread(r, squares):
            deltas = [end[lo + r, tile[x], :] - means[x] for x in range(size_x)]
            return tuple(s + d * d for s, d in zip(squares, deltas))

        squares = lax.fori_loop(0, ny, spread, (zero,) * size_x)
        share = ny / (done + ny)
        for x in range(size_x):
            if done == 0:
                moments[0, 0, tile[x], :] = means[x]
                moments[0, 1, tile[x], :] = squares[x]
            else:
                delta = means[x] - moments[0, 0, tile[x], :]
                moments[0, 0, tile[x], :] += delta * share
                moments[0, 1, tile[x], :] += squares[x] + delta * delta * (done * share)
        done += ny

    for r in range(1, rows):
        moment_copy(r).start()
    at = 0
    for devices, source in ((cols, xsend), (slabs, zsend)):
        for side in range(1 if devices == 2 else 2):
            sides = pl.ds(side, 2 if devices == 2 else 1)
            sent = source.at[:, sides]
            pltpu.make_async_copy(sent, sent, face_send.at[at]).wait()
            at += 1
    sent = fbuf.at[0, pl.ds(0, 2 * STEPS)]
    pltpu.make_async_copy(sent, sent, row_send).wait()
    for r in range(1, rows):
        moment_copy(r).wait()


def finish(size_y, pieces, end, moments, standardized_hbm, end_hbm, out, end_sem, out_sem):
    rows = moments.shape[0]
    ny = size_y // pieces
    copy_end = pltpu.make_async_copy(end, end_hbm, end_sem)
    copy_end.start()

    parts = [moments[r, 0] for r in range(rows)]
    mean = sum(parts[1:], parts[0]) * (1.0 / rows)
    square = sum([moments[r, 1] for r in range(1, rows)], moments[0, 1])
    for p in parts:
        square = square + size_y * ((p - mean) * (p - mean))
    scale = lax.rsqrt(square * (1.0 / (rows * size_y)) + 0.0001)

    def store(j):
        return pltpu.make_async_copy(out.at[pl.ds(j * ny, ny)], standardized_hbm.at[pl.ds(j * ny, ny)], out_sem)

    for j in range(pieces):
        @pl.loop(0, ny)
        def _(r):
            y = j * ny + r
            out[y] = (end[y] - mean) * scale

        store(j).start()

    pltpu.make_async_copy(out, standardized_hbm, out_sem).wait()
    copy_end.wait()


def local(dims, field_values, crowding):
    shape = field_values.shape
    size_y, size_x, size_z, levels = shape
    rows, cols, slabs = dims
    most = max(map(len, pieces_of(size_y)))
    links = sum(1 if devices == 2 else 2 for devices in (cols, slabs))
    chunks = next(n for n in (4, 3, 6, 2, 1) if size_y % n == 0)
    flat = (size_y, size_x * size_z, levels)
    dma = pltpu.SemaphoreType.DMA
    held = (flat, (rows, 2) + flat[1:])
    out = tuple(pltpu.VMEM(each, jnp.float32) for each in held)
    vmem_spec = pl.BlockSpec(memory_space=pltpu.VMEM)
    any_spec = pl.BlockSpec(memory_space=pl.ANY)
    field_end, moments = pl.pallas_call(
        functools.partial(kernel, (rows, cols, slabs, size_y, size_x, size_z)),
        out_shape=out,
        in_specs=[any_spec] * 2,
        out_specs=(vmem_spec,) * 2,
        scratch_shapes=[
            pltpu.VMEM((STEPS, size_y + 2, size_x * size_z, levels), jnp.float32),
            pltpu.VMEM(flat, jnp.float32),
            pltpu.VMEM((STEPS, 2, size_y, size_z, levels), jnp.float32),
            pltpu.VMEM((STEPS, 2, size_y, size_z, levels), jnp.float32),
            pltpu.VMEM((STEPS, 2, size_y, size_x, levels), jnp.float32),
            pltpu.VMEM((STEPS, 2, size_y, size_x, levels), jnp.float32),
            dma((len(pieces_of(size_y)[0]),)),
            dma,
            dma((links,)),
            dma((2, most, links)),
            dma,
            dma((2, 2)),
            dma((rows - 1,)),
            dma((rows - 1,)),
        ],
        compiler_params=pltpu.CompilerParams(
            collective_id=0, has_side_effects=True, vmem_limit_bytes=58 * 1024 * 1024),
    )(field_values.reshape(flat), crowding.reshape(flat))
    whole = jax.ShapeDtypeStruct(flat, jnp.float32)
    standardized, field_end = pl.pallas_call(
        functools.partial(finish, size_y, chunks),
        out_shape=(whole, whole),
        in_specs=[vmem_spec] * 2,
        out_specs=(any_spec,) * 2,
        scratch_shapes=[pltpu.VMEM(flat, jnp.float32), dma, dma],
        compiler_params=pltpu.CompilerParams(vmem_limit_bytes=16 * 1024 * 1024),
    )(*(pltpu.with_memory_space_constraint(each, pltpu.VMEM) for each in (field_end, moments)))
    return standardized.reshape(shape), field_end.reshape(shape)


def solution(mesh):
    spec = P(("site", "rows"), "cols", "slabs", None)
    dims = tuple(mesh.shape[axis] for axis in ("rows", "cols", "slabs"))
    return jax.shard_map(
        functools.partial(local, dims), mesh=mesh,
        in_specs=(spec, spec), out_specs=(spec, spec), check_vma=False)
```

time: 114 us -> 112 us (0.982)
  Pallas kernels: 113 us -> 111 us
    pallas_call x1, Pallas kernels: 110 us -> 108 us  [local(): pl.pallas_call(functools.partial(kernel, (rows, cols, slabs, size_y, size...]
where the time goes in v2:
time: 112 us; the launch traced here: 111 us
  Pallas kernels  111 us (99%)
    pallas_call x1, Pallas kernels, local(): pl.pallas_call(functools.partial(kernel, (rows, cols, slabs, size_y, size...  108 us
    pallas_call x1, Pallas kernels, local(): pl.pallas_call(functools.partial(finish, size_y, chunks), out_shape=(whol...  2.69 us

profile of v2, /device:TPU:0, one launch (start us, length us, event | category | flops | bytes accessed | tf_op | source)
XLA Modules:
  0.0 111.4 jit_solution(4905113810304044095)
XLA Ops:
  0.6 108.1 %shard_map.41 = (f32[96,64,128]{2,1,0:T(8,128)S(1)}, f32[2,2,64,128]{3,2,1,0:T(8,128)S(1)}) custom-call(f32[96,64,128]{2,1,0:T(8,128)} %bitcast.4, f32[96,64,128]{2,1,0:T(8,128)} %bitcast.5), custom_call_target="tpu_custom_call" | custom-call | tf_op jit(solution)/shard_map/pallas_call | solution.py:258
  108.7 2.7 %shard_map.42 = (f32[96,64,128]{2,1,0:T(8,128)}, f32[96,64,128]{2,1,0:T(8,128)}) custom-call(f32[96,64,128]{2,1,0:T(8,128)S(1)} %get-tuple-element.6.end, f32[2,2,64,128]{3,2,1,0:T(8,128)S(1)} %get-tuple-element.7.moments), custom_call_target="tpu_custom_call" | custom-call | tf_op jit(solution)/shard_map/pallas_call | solution.py:283

commit v3 on v2

--- a/solution.py
+++ b/solution.py
@@ -17,16 +17,11 @@
 
 
 def pieces_of(size_y):
-    small = max(1, size_y // 12)
-
-    def cut(*ends):
-        ends = sorted({e for e in ends if 0 < e < size_y} | {0, size_y})
+    def cut(*parts):
+        ends = sorted({size_y * part // 24 for part in parts} | {0, size_y})
         return tuple((lo, hi - lo) for lo, hi in zip(ends, ends[1:]))
 
-    middle = tuple(size_y * i // 2 for i in range(1, 2))
-    first = cut(small, *middle)
-    last = cut(size_y - small, *middle)
-    return (first,) + (cut(*middle),) * (STEPS - 2) + (last,)
+    return (cut(2, 8, 16),) + (cut(8, 16),) * (STEPS - 2) + (cut(10, 17, 21, 23),)
 
 
 def kernel(dims, f_hbm, c_hbm, end, moments, fbuf, cbuf, xsend, xrecv, zsend, zrecv,

time: 112 us -> 111 us (level)
  no operation moved by 1% of the time
where the time goes in v3:
time: 111 us
  Pallas kernels  110 us (99%)
    pallas_call x1, Pallas kernels, local(): pl.pallas_call(functools.partial(kernel, (rows, cols, slabs, size_y, size...  107 us
    pallas_call x1, Pallas kernels, local(): pl.pallas_call(functools.partial(finish, size_y, chunks), out_shape=(whol...  2.69 us

profile of v3, /device:TPU:0, one launch (start us, length us, event | category | flops | bytes accessed | tf_op | source)
XLA Modules:
  0.0 110.8 jit_solution(11948762081853655735)
XLA Ops:
  0.6 107.5 %shard_map.41 = (f32[96,64,128]{2,1,0:T(8,128)S(1)}, f32[2,2,64,128]{3,2,1,0:T(8,128)S(1)}) custom-call(f32[96,64,128]{2,1,0:T(8,128)} %bitcast.4, f32[96,64,128]{2,1,0:T(8,128)} %bitcast.5), custom_call_target="tpu_custom_call" | custom-call | tf_op jit(solution)/shard_map/pallas_call | solution.py:253
  108.1 2.7 %shard_map.42 = (f32[96,64,128]{2,1,0:T(8,128)}, f32[96,64,128]{2,1,0:T(8,128)}) custom-call(f32[96,64,128]{2,1,0:T(8,128)S(1)} %get-tuple-element.6.end, f32[2,2,64,128]{3,2,1,0:T(8,128)S(1)} %get-tuple-element.7.moments), custom_call_target="tpu_custom_call" | custom-call | tf_op jit(solution)/shard_map/pallas_call | solution.py:278

commit v4 on v3

--- a/solution.py
+++ b/solution.py
@@ -24,10 +24,11 @@
     return (cut(2, 8, 16),) + (cut(8, 16),) * (STEPS - 2) + (cut(10, 17, 21, 23),)
 
 
-def kernel(dims, f_hbm, c_hbm, end, moments, fbuf, cbuf, xsend, xrecv, zsend, zrecv,
-           load_sem, crowd_sem, face_send, face_recv, row_send, row_recv, mom_send, mom_recv):
+def kernel(dims, f_hbm, c_hbm, end, moments, fbuf, cbuf, fsend, frecv,
+           load_sem, face_send, face_recv, core_send, row_recv, mom_recv):
     rows, cols, slabs, size_y, size_x, size_z = dims
     pieces = pieces_of(size_y)
+    common = min(map(len, pieces))
     levels = f_hbm.shape[-1]
     x_next = ring("cols", cols)
     z_next = ring("slabs", slabs)
@@ -35,16 +36,24 @@
     y_next = ring("rows", rows)
     tile = [pl.ds(x * size_z, size_z) for x in range(size_x)]
 
+    x_part = [pl.ds(side * size_z, size_z) for side in (0, 1)]
+    z_first = [2 * size_z + side * size_x for side in (0, 1)]
+    z_part = [pl.ds(first, size_x) for first in z_first]
+
+    def arrived(k, p):
+        return (k % 2) * common + p if p < common else 2 * common + p - common
+
     def faces(k, p):
         copies = []
         at_rows = pl.ds(*pieces[k][p])
-        for axis, devices, source, target, peers in (
-                ("cols", cols, xsend, xrecv, x_next), ("slabs", slabs, zsend, zrecv, z_next)):
+        for axis, devices, parts, whole, peers in (
+                ("cols", cols, x_part, pl.ds(0, 2 * size_z), x_next),
+                ("slabs", slabs, z_part, pl.ds(2 * size_z, 2 * size_x), z_next)):
             for side in range(1 if devices == 2 else 2):
-                sides = pl.ds(side, 2 if devices == 2 else 1)
+                part = whole if devices == 2 else parts[side]
                 copies.append(pltpu.make_async_remote_copy(
-                    src_ref=source.at[k, sides, at_rows], dst_ref=target.at[k, sides, at_rows],
-                    send_sem=face_send.at[len(copies)], recv_sem=face_recv.at[k % 2, p, len(copies)],
+                    src_ref=fsend.at[k, at_rows, part], dst_ref=frecv.at[k, at_rows, part],
+                    send_sem=face_send, recv_sem=face_recv.at[arrived(k, p)],
                     device_id={axis: peers[side]}, device_id_type=MESH))
         return copies
 
@@ -52,19 +61,22 @@
         return pltpu.make_async_remote_copy(
             src_ref=fbuf.at[k, size_y if side == 0 else 1],
             dst_ref=fbuf.at[k, 0 if side == 0 else size_y + 1],
-            send_sem=row_send, recv_sem=row_recv.at[k % 2, side],
+            send_sem=core_send, recv_sem=row_recv.at[k % 2],
             device_id={"rows": y_next[side]}, device_id_type=MESH)
+
+    def wait_bytes(ref, sem):
+        pltpu.make_async_copy(ref, ref, sem).wait()
 
     def load(p):
         lo, ny = pieces[0][p]
-        return pltpu.make_async_copy(f_hbm.at[pl.ds(lo, ny)], fbuf.at[0, pl.ds(lo + 1, ny)], load_sem.at[p])
-
-    crowd = pltpu.make_async_copy(c_hbm, cbuf, crowd_sem)
+        return pltpu.make_async_copy(f_hbm.at[pl.ds(lo, ny)], fbuf.at[0, pl.ds(lo + 1, ny)], load_sem.at[p % 2])
+
+    crowd = pltpu.make_async_copy(c_hbm, cbuf, load_sem.at[0])
 
     def moment_copy(r):
         return pltpu.make_async_remote_copy(
             src_ref=moments.at[0], dst_ref=moments.at[r],
-            send_sem=mom_send.at[r - 1], recv_sem=mom_recv.at[r - 1],
+            send_sem=core_send, recv_sem=mom_recv.at[r - 1],
             device_id={"rows": lax.rem(lax.axis_index("rows") + r, rows)}, device_id_type=MESH)
 
     def start_faces(k, p):
@@ -79,9 +91,9 @@
             y = lo + r
             for side in (0, 1):
                 first = size_z - 1 if side == 0 else 0
-                zsend[k, side, y] = fbuf[k, y + 1, pl.ds(first, size_x, stride=size_z), :]
+                fsend[k, y, z_part[side]] = fbuf[k, y + 1, pl.ds(first, size_x, stride=size_z), :]
                 if not k:
-                    xsend[k, side, y] = fbuf[k, y + 1, tile[size_x - 1 if side == 0 else 0], :]
+                    fsend[k, y, x_part[side]] = fbuf[k, y + 1, tile[size_x - 1 if side == 0 else 0], :]
 
         for copy in copies[x_copies if k else 0:]:
             copy.start()
@@ -95,12 +107,9 @@
 
     def wait_recv(k, p):
         lo, ny = pieces[k][p]
-        for copy in faces(k, p):
-            copy.wait_recv()
-        if lo == 0:
-            y_copy(k, 0).wait_recv()
-        if lo + ny == size_y:
-            y_copy(k, 1).wait_recv()
+        wait_bytes(frecv.at[k, pl.ds(lo, ny)], face_recv.at[arrived(k, p)])
+        if p == 0:
+            wait_bytes(fbuf.at[k, pl.ds(0, 2)], row_recv.at[k % 2])
 
     at_z = lax.broadcasted_iota(jnp.int32, (size_z, levels), 0)
 
@@ -113,10 +122,10 @@
             out = []
             for x in range(size_x):
                 m = mid[x]
-                below = mid[x - 1] if x > 0 else xrecv[k, 0, y]
-                above = mid[x + 1] if x < size_x - 1 else xrecv[k, 1, y]
-                z_lo = jnp.broadcast_to(zrecv[k, 0, y, pl.ds(x, 1), :], m.shape)
-                z_hi = jnp.broadcast_to(zrecv[k, 1, y, pl.ds(x, 1), :], m.shape)
+                below = mid[x - 1] if x > 0 else frecv[k, y, x_part[0]]
+                above = mid[x + 1] if x < size_x - 1 else frecv[k, y, x_part[1]]
+                z_lo = jnp.broadcast_to(frecv[k, y, pl.ds(z_first[0] + x, 1), :], m.shape)
+                z_hi = jnp.broadcast_to(frecv[k, y, pl.ds(z_first[1] + x, 1), :], m.shape)
                 left = jnp.where(at_z == 0, z_lo, pltpu.roll(m, 1, 0))
                 right = jnp.where(at_z == size_z - 1, z_hi, pltpu.roll(m, size_z - 1, 0))
                 near = (fbuf[k, y, tile[x], :] + fbuf[k, y + 2, tile[x], :]) + (below + above) + (left + right)
@@ -126,9 +135,9 @@
                 else:
                     fbuf[k + 1, y + 1, tile[x], :] = new
                     if x == size_x - 1:
-                        xsend[k + 1, 0, y] = new
+                        fsend[k + 1, y, x_part[0]] = new
                     if x == 0:
-                        xsend[k + 1, 1, y] = new
+                        fsend[k + 1, y, x_part[1]] = new
                 out.append(new)
             return tuple(s + o for s, o in zip(sums, out)) if sums else ()
 
@@ -150,9 +159,9 @@
     pl.semaphore_wait(barrier, count)
 
     for p in range(len(pieces[0])):
+        load(p).wait()
         if p + 2 < len(pieces[0]):
             load(p + 2).start()
-        load(p).wait()
         start_faces(0, p)
         start_y(0, p)
     crowd.start()
@@ -196,17 +205,10 @@
 
     for r in range(1, rows):
         moment_copy(r).start()
-    at = 0
-    for devices, source in ((cols, xsend), (slabs, zsend)):
-        for side in range(1 if devices == 2 else 2):
-            sides = pl.ds(side, 2 if devices == 2 else 1)
-            sent = source.at[:, sides]
-            pltpu.make_async_copy(sent, sent, face_send.at[at]).wait()
-            at += 1
-    sent = fbuf.at[0, pl.ds(0, 2 * STEPS)]
-    pltpu.make_async_copy(sent, sent, row_send).wait()
+    wait_bytes(frecv, face_send)
     for r in range(1, rows):
-        moment_copy(r).wait()
+        moment_copy(r).wait_recv()
+    wait_bytes(fbuf.at[0, pl.ds(0, 2 * STEPS + 2 * (rows - 1))], core_send)
 
 
 def finish(size_y, pieces, end, moments, standardized_hbm, end_hbm, out, end_sem, out_sem):
@@ -241,8 +243,8 @@
     shape = field_values.shape
     size_y, size_x, size_z, levels = shape
     rows, cols, slabs = dims
-    most = max(map(len, pieces_of(size_y)))
-    links = sum(1 if devices == 2 else 2 for devices in (cols, slabs))
+    counts = sorted(map(len, pieces_of(size_y)))
+    arrivals = counts[0] + counts[-1]
     chunks = next(n for n in (4, 3, 6, 2, 1) if size_y % n == 0)
     flat = (size_y, size_x * size_z, levels)
     dma = pltpu.SemaphoreType.DMA
@@ -258,17 +260,13 @@
         scratch_shapes=[
             pltpu.VMEM((STEPS, size_y + 2, size_x * size_z, levels), jnp.float32),
             pltpu.VMEM(flat, jnp.float32),
-            pltpu.VMEM((STEPS, 2, size_y, size_z, levels), jnp.float32),
-            pltpu.VMEM((STEPS, 2, size_y, size_z, levels), jnp.float32),
-            pltpu.VMEM((STEPS, 2, size_y, size_x, levels), jnp.float32),
-            pltpu.VMEM((STEPS, 2, size_y, size_x, levels), jnp.float32),
-            dma((len(pieces_of(size_y)[0]),)),
+            pltpu.VMEM((STEPS, size_y, 2 * (size_z + size_x), levels), jnp.float32),
+            pltpu.VMEM((STEPS, size_y, 2 * (size_z + size_x), levels), jnp.float32),
+            dma((2,)),
             dma,
-            dma((links,)),
-            dma((2, most, links)),
+            dma((arrivals,)),
             dma,
-            dma((2, 2)),
-            dma((rows - 1,)),
+            dma((2,)),
             dma((rows - 1,)),
         ],
         compiler_params=pltpu.CompilerParams(

time: 111 us -> 111 us (level)
  no operation moved by 1% of the time
where the time goes in v4:
time: 111 us
  Pallas kernels  110 us (99%)
    pallas_call x1, Pallas kernels, local(): pl.pallas_call(functools.partial(kernel, (rows, cols, slabs, size_y, size...  107 us
    pallas_call x1, Pallas kernels, local(): pl.pallas_call(functools.partial(finish, size_y, chunks), out_shape=(whol...  2.69 us

profile of v4, /device:TPU:0, one launch (start us, length us, event | category | flops | bytes accessed | tf_op | source)
XLA Modules:
  0.0 110.6 jit_solution(10564421507651903769)
XLA Ops:
  0.6 107.3 %shard_map.41 = (f32[96,64,128]{2,1,0:T(8,128)S(1)}, f32[2,2,64,128]{3,2,1,0:T(8,128)S(1)}) custom-call(f32[96,64,128]{2,1,0:T(8,128)} %bitcast.4, f32[96,64,128]{2,1,0:T(8,128)} %bitcast.5), custom_call_target="tpu_custom_call" | custom-call | tf_op jit(solution)/shard_map/pallas_call | solution.py:255
  107.9 2.7 %shard_map.42 = (f32[96,64,128]{2,1,0:T(8,128)}, f32[96,64,128]{2,1,0:T(8,128)}) custom-call(f32[96,64,128]{2,1,0:T(8,128)S(1)} %get-tuple-element.6.end, f32[2,2,64,128]{3,2,1,0:T(8,128)S(1)} %get-tuple-element.7.moments), custom_call_target="tpu_custom_call" | custom-call | tf_op jit(solution)/shard_map/pallas_call | solution.py:276

commit v5 on v4

--- a/solution.py
+++ b/solution.py
@@ -25,7 +25,7 @@
 
 
 def kernel(dims, f_hbm, c_hbm, end, moments, fbuf, cbuf, fsend, frecv,
-           load_sem, face_send, face_recv, core_send, row_recv, mom_recv):
+           load_sem, face_send, face_recv, core_send, row_recv):
     rows, cols, slabs, size_y, size_x, size_z = dims
     pieces = pieces_of(size_y)
     common = min(map(len, pieces))
@@ -72,12 +72,6 @@
         return pltpu.make_async_copy(f_hbm.at[pl.ds(lo, ny)], fbuf.at[0, pl.ds(lo + 1, ny)], load_sem.at[p % 2])
 
     crowd = pltpu.make_async_copy(c_hbm, cbuf, load_sem.at[0])
-
-    def moment_copy(r):
-        return pltpu.make_async_remote_copy(
-            src_ref=moments.at[0], dst_ref=moments.at[r],
-            send_sem=core_send, recv_sem=mom_recv.at[r - 1],
-            device_id={"rows": lax.rem(lax.axis_index("rows") + r, rows)}, device_id_type=MESH)
 
     def start_faces(k, p):
         lo, ny = pieces[k][p]
@@ -195,37 +189,38 @@
         share = ny / (done + ny)
         for x in range(size_x):
             if done == 0:
-                moments[0, 0, tile[x], :] = means[x]
-                moments[0, 1, tile[x], :] = squares[x]
+                moments[0, tile[x], :] = means[x]
+                moments[1, tile[x], :] = squares[x]
             else:
-                delta = means[x] - moments[0, 0, tile[x], :]
-                moments[0, 0, tile[x], :] += delta * share
-                moments[0, 1, tile[x], :] += squares[x] + delta * delta * (done * share)
+                delta = means[x] - moments[0, tile[x], :]
+                moments[0, tile[x], :] += delta * share
+                moments[1, tile[x], :] += squares[x] + delta * delta * (done * share)
         done += ny
 
-    for r in range(1, rows):
-        moment_copy(r).start()
     wait_bytes(frecv, face_send)
-    for r in range(1, rows):
-        moment_copy(r).wait_recv()
-    wait_bytes(fbuf.at[0, pl.ds(0, 2 * STEPS + 2 * (rows - 1))], core_send)
-
-
-def finish(size_y, pieces, end, moments, standardized_hbm, end_hbm, out, end_sem, out_sem):
-    rows = moments.shape[0]
+    wait_bytes(fbuf.at[0, pl.ds(0, 2 * STEPS)], core_send)
+
+
+def keep(head, end, end_hbm, end_sem):
+    at = pl.ds(0, head)
+    copy_end = pltpu.make_async_copy(end.at[at], end_hbm.at[at], end_sem)
+    copy_end.start()
+    copy_end.wait()
+
+
+def finish(size_y, head, pieces, kept_hbm, end, *refs):
+    moments, (standardized_hbm, end_hbm, out, out_sem, end_sem) = refs[:-5], refs[-5:]
+    rows = len(moments)
+    at = pl.ds(head, size_y - head)
+    copy_end = pltpu.make_async_copy(end.at[at], end_hbm.at[at], end_sem)
+    copy_end.start()
     ny = size_y // pieces
-    copy_end = pltpu.make_async_copy(end, end_hbm, end_sem)
-    copy_end.start()
-
-    parts = [moments[r, 0] for r in range(rows)]
+    parts = [m[0] for m in moments]
     mean = sum(parts[1:], parts[0]) * (1.0 / rows)
-    square = sum([moments[r, 1] for r in range(1, rows)], moments[0, 1])
+    square = sum([m[1] for m in moments[1:]], moments[0][1])
     for p in parts:
         square = square + size_y * ((p - mean) * (p - mean))
     scale = lax.rsqrt(square * (1.0 / (rows * size_y)) + 0.0001)
-
-    def store(j):
-        return pltpu.make_async_copy(out.at[pl.ds(j * ny, ny)], standardized_hbm.at[pl.ds(j * ny, ny)], out_sem)
 
     for j in range(pieces):
         @pl.loop(0, ny)
@@ -233,8 +228,8 @@
             y = j * ny + r
             out[y] = (end[y] - mean) * scale
 
-        store(j).start()
-
+        at = pl.ds(j * ny, ny)
+        pltpu.make_async_copy(out.at[at], standardized_hbm.at[at], out_sem).start()
     pltpu.make_async_copy(out, standardized_hbm, out_sem).wait()
     copy_end.wait()
 
@@ -248,7 +243,7 @@
     chunks = next(n for n in (4, 3, 6, 2, 1) if size_y % n == 0)
     flat = (size_y, size_x * size_z, levels)
     dma = pltpu.SemaphoreType.DMA
-    held = (flat, (rows, 2) + flat[1:])
+    held = (flat, (2,) + flat[1:])
     out = tuple(pltpu.VMEM(each, jnp.float32) for each in held)
     vmem_spec = pl.BlockSpec(memory_space=pltpu.VMEM)
     any_spec = pl.BlockSpec(memory_space=pl.ANY)
@@ -267,20 +262,31 @@
             dma((arrivals,)),
             dma,
             dma((2,)),
-            dma((rows - 1,)),
         ],
         compiler_params=pltpu.CompilerParams(
             collective_id=0, has_side_effects=True, vmem_limit_bytes=58 * 1024 * 1024),
     )(field_values.reshape(flat), crowding.reshape(flat))
+    def held_in_vmem(each):
+        return pltpu.with_memory_space_constraint(each, pltpu.VMEM)
+
     whole = jax.ShapeDtypeStruct(flat, jnp.float32)
+    head = size_y * 5 // 8
+    small = pltpu.CompilerParams(vmem_limit_bytes=16 * 1024 * 1024)
+    others = [lax.ppermute(moments, "rows", [(i, (i + r) % rows) for i in range(rows)]) for r in range(1, rows)]
+    field_in_vmem = held_in_vmem(field_end)
+    kept = pl.pallas_call(
+        functools.partial(keep, head), out_shape=whole, in_specs=[vmem_spec], out_specs=any_spec, scratch_shapes=[dma], compiler_params=small,
+        cost_estimate=pl.CostEstimate(flops=2 * 10 ** 8, bytes_accessed=0, transcendentals=0),
+    )(field_in_vmem)
     standardized, field_end = pl.pallas_call(
-        functools.partial(finish, size_y, chunks),
+        functools.partial(finish, size_y, head, chunks),
         out_shape=(whole, whole),
-        in_specs=[vmem_spec] * 2,
+        in_specs=[any_spec] + [vmem_spec] * (1 + rows),
         out_specs=(any_spec,) * 2,
         scratch_shapes=[pltpu.VMEM(flat, jnp.float32), dma, dma],
-        compiler_params=pltpu.CompilerParams(vmem_limit_bytes=16 * 1024 * 1024),
-    )(*(pltpu.with_memory_space_constraint(each, pltpu.VMEM) for each in (field_end, moments)))
+        input_output_aliases={0: 1},
+        compiler_params=small,
+    )(kept, field_in_vmem, held_in_vmem(moments), *others)
     return standardized.reshape(shape), field_end.reshape(shape)
 
 

time: 111 us -> 111 us (level)
    pallas_call x1 -> x2, Pallas kernels: 2.69 us -> 3.35 us  [the longest x1 2.07 us: local(): pl.pallas_call(functools.partial(finish, size_y, head, chunks), out_shape...]
  transfers between devices with their start and end apart: 0 -> 1, of which waited for: 0 -> 0; matrix products, arithmetic and copies ran while one was open for 0% -> 0% of each run, Pallas kernels for 0% -> 1%
where the time goes in v5:
time: 111 us; the launch traced here: 110 us
  Pallas kernels  110 us (99%)
    pallas_call x1, Pallas kernels, local(): pl.pallas_call(functools.partial(kernel, (rows, cols, slabs, size_y, size...  106 us
  transfers between devices with their start and end apart: 1, of which 0 were waited for; matrix products, arithmetic and copies ran while one was open for 0% of the time, Pallas kernels for 1%

profile of v5, /device:TPU:0, one launch (start us, length us, event | category | flops | bytes accessed | tf_op | source)
XLA Modules:
  0.0 110.4 jit_solution(16573279098532568561)
XLA Ops:
  0.6 106.4 %shard_map.41 = (f32[96,64,128]{2,1,0:T(8,128)S(1)}, f32[2,64,128]{2,1,0:T(8,128)S(1)}) custom-call(f32[96,64,128]{2,1,0:T(8,128)} %bitcast.5, f32[96,64,128]{2,1,0:T(8,128)} %bitcast.6), custom_call_target="tpu_custom_call" | custom-call | tf_op jit(solution)/shard_map/pallas_call | solution.py:250
  107.0 0.1 collective-permute-start
  107.1 1.3 %shard_map.42.kept_hbm = f32[96,64,128]{2,1,0:T(8,128)} custom-call(f32[96,64,128]{2,1,0:T(8,128)S(1)} %get-tuple-element.6.end), custom_call_target="tpu_custom_call" | custom-call | flops 200000000 | tf_op jit(solution)/shard_map/pallas_call | solution.py:277
  108.4 0.0 collective-permute-done.refs_1_
  108.4 2.1 %shard_map.43 = (f32[96,64,128]{2,1,0:T(8,128)}, f32[96,64,128]{2,1,0:T(8,128)}) custom-call(f32[96,64,128]{2,1,0:T(8,128)} %shard_map.42.kept_hbm, f32[96,64,128]{2,1,0:T(8,128)S(1)} %get-tuple-element.6.end, f32[2,64,128]{2,1,0:T(8,128)S(1)} %get-tuple-element.7.refs_0_, ...), custom_call_target="tpu_custom_call", output_to_operand_aliasing={{1}: (0, {})} | custom-call | tf_op jit(solution)/shard_map/pallas_call | solution.py:281
Async XLA Ops:
  107.0 1.4 %collective-permute-start = (f32[2,64,128]{2,1,0:T(8,128)S(1)}, f32[2,64,128]{2,1,0:T(8,128)S(1)}, u32[]{:S(2)}, u32[]{:S(2)}) collective-permute-start(f32[2,64,128]{2,1,0:T(8,128)S(1)} %get-tuple-element.7.refs_0_), channel_id=1, source_target_pairs={{0,16},{16,0},{1,17},{17,1},{2,18},{18,2},{3,19},{19,3},{4,20},{20... | collective-permute-start | bytes 196616 | tf_op jit(solution)/shard_map/ppermute | solution.py:275
